TPU v7x, 32 devices: a whole 2x2x4 slice. The times are simulated.
32 devices in a mesh: basin: 2 (over x), recv: 8 (over z, y), src: 2 (over core).
Axes of the slice: x: 2, y: 2, z: 4, core: 2. Of those that a mesh axis runs over, the one named last changes fastest.
Arguments:
- positions: float32 [3, 4096], P(None, ('basin', 'recv', 'src')), parts along dimension 1, may hold values from -1.1 to 1.1, as said below
- normals: float32 [3, 4096], P(None, ('basin', 'recv', 'src')), parts along dimension 1, may hold values from -1 to 1, as said below
- area: float32 [4096], P(('basin', 'recv', 'src')), parts along dimension 0, may hold values from 0.0009765625 to 0.0078125
- albedo: float32 [4096], P(('basin', 'recv', 'src')), parts along dimension 0, may hold values from 0.1 to 0.6
- conductivity: float32 [4096], P(('basin', 'recv', 'src')), parts along dimension 0, may hold values from 0.05 to 0.4
- soil: float32 [32, 4096], P(None, ('basin', 'recv', 'src')), parts along dimension 1, may hold values from 0.5 to 1.2
- sun_tan: float32 [16], replicated, may hold values from 0.05 to 2
- samples: int32 [32, 32], P(('basin', 'recv', 'src')), parts along dimension 0, may hold values from 1 to 2047
- occupancy: int32 [32, 16], P('basin'), parts along dimension 0, may hold values 0 or 1
Outputs:
- soil_final: float32 [32, 4096], P(None, ('basin', 'recv', 'src')), parts along dimension 1
- bounce: float32 [16, 4096], P(None, ('basin', 'recv', 'src')), parts along dimension 1
There are 2 independent parts, one for each index of `basin`. A program takes and returns all parts, laid end to end along the dimension named above; an argument that names none is the same for every part. Nothing has to cross between parts.
Inputs may be any that keep to these rules, and one draw needn't show every extreme that they name: `positions`: facets lie on a bowl below z = 0. `normals`: each column has unit length.
All inputs are finite; a program needn't handle non-finite values.
Results may differ from a plain program's by a relative error of at most 0.0003.
Values may be sent and summed in bfloat16 or wider, within the bound.
A program may use at most 64 MiB of HBM per device.

v0:
```python
import math

import jax
import jax.numpy as jnp
from jax import lax
from jax.sharding import PartitionSpec as P

solar_flux = 2.0
emissivity = 0.9
surface_gain = 0.1
shade_width = 0.1
reach_offset = 0.05


def partner(value, axis, apart):
    mask = 2**apart
    pairs = [(source, source ^ mask) for source in range(lax.axis_size(axis))]
    return lax.ppermute(value, axis, pairs)


def fourth(value):
    square = value * value
    return square * square


def rotate(values, shift):
    count = values.shape[0]
    doubled = jnp.concatenate([values, values], 0)
    return lax.dynamic_slice_in_dim(doubled, shift, count, 0)


def profile_max(coords, offsets):
    px, py, pz = (coords[0], coords[1], coords[2])
    count = px.shape[0]

    def sweep(best, shift):
        delta_x = rotate(px, shift) - px
        delta_y = rotate(py, shift) - py
        reach = jnp.sqrt(delta_x * delta_x + delta_y * delta_y) + reach_offset
        slope = (rotate(pz, shift) - pz) / reach
        return (jnp.maximum(best, slope), None)

    start = jnp.full((count,), -1e30, jnp.float32)
    best, unused = lax.scan(sweep, start, offsets)
    return best


def horizons(coords, samples):
    return lax.map(lambda offsets: profile_max(coords, offsets), samples)


def sunlight(facing, sun_tan, horizon):
    count = sun_tan.shape[0]
    angle = 2.0 * math.pi * jnp.arange(count, dtype=jnp.float32) / count
    elevation = jnp.arctan(sun_tan)
    sun_x = jnp.cos(elevation) * jnp.cos(angle)
    sun_y = jnp.cos(elevation) * jnp.sin(angle)
    sun_z = jnp.sin(elevation)
    incidence = (
        sun_x[:, None] * facing[0][None, :]
        + sun_y[:, None] * facing[1][None, :]
        + sun_z[:, None] * facing[2][None, :]
    )
    shade = jax.nn.sigmoid((sun_tan[:, None] - horizon) / shade_width)
    return solar_flux * jnp.maximum(incidence, 0.0) * shade


def conduct(soil, direct, bounce, albedo, conductivity):

    def advance(temps, inputs):
        light, scattered = inputs
        grad = temps[1:] - temps[:-1]
        edge = jnp.zeros((1, temps.shape[1]), jnp.float32)
        change = jnp.concatenate([grad, edge], 0) - jnp.concatenate([edge, grad], 0)
        temps = temps + conductivity[None, :] * change
        absorbed = (1.0 - albedo) * (light + scattered)
        top = temps[0] + surface_gain * (absorbed - emissivity * fourth(temps[0]))
        return (jnp.concatenate([top[None, :], temps[1:]], 0), None)

    final, unused = lax.scan(advance, soil, (direct, bounce))
    return final


def view_tile(src_pos, src_nrm, src_area, src_ids, rec_pos, rec_nrm, mask_rows, width):
    onehot = (src_ids[:, None] == jnp.arange(mask_rows.shape[1], dtype=jnp.int32)[None, :]).astype(
        jnp.float32
    )
    weight = jnp.dot(
        onehot, mask_rows.T, preferred_element_type=jnp.float32, precision=lax.Precision.HIGHEST
    )
    weight = jnp.repeat(weight, width, axis=1)
    delta_x = src_pos[0][:, None] - rec_pos[0][None, :]
    delta_y = src_pos[1][:, None] - rec_pos[1][None, :]
    delta_z = src_pos[2][:, None] - rec_pos[2][None, :]
    facing = jnp.maximum(
        rec_nrm[0][None, :] * delta_x
        + rec_nrm[1][None, :] * delta_y
        + rec_nrm[2][None, :] * delta_z,
        0.0,
    )
    toward = jnp.maximum(
        -(
            src_nrm[0][:, None] * delta_x
            + src_nrm[1][:, None] * delta_y
            + src_nrm[2][:, None] * delta_z
        ),
        0.0,
    )
    spread = delta_x * delta_x + delta_y * delta_y + delta_z * delta_z + src_area[:, None]
    return (facing * toward * src_area[:, None] * weight / (math.pi * spread * spread)).astype(
        jnp.bfloat16
    )


def make_fold(src_pos, src_nrm, src_area, block_of, rec_pos, rec_nrm, mask_rows, width):

    def add_tile(carry, segment, begin, count):
        ids = block_of(begin + jnp.arange(count, dtype=jnp.int32))
        pos = lax.dynamic_slice_in_dim(src_pos, begin, count, 1)
        nrm = lax.dynamic_slice_in_dim(src_nrm, begin, count, 1)
        sizes = lax.dynamic_slice_in_dim(src_area, begin, count, 0)
        view = view_tile(pos, nrm, sizes, ids, rec_pos, rec_nrm, mask_rows, width)
        return carry + jnp.dot(segment, view, preferred_element_type=jnp.float32)

    def fold(carry, piece, start):
        count = piece.shape[1]

        def step_once(total, number):
            offset = number * width
            segment = lax.dynamic_slice_in_dim(piece, offset, width, 1)
            return (add_tile(total, segment, offset, width), None)

        total, unused = lax.scan(step_once, carry, jnp.arange(count // width, dtype=jnp.int32))
        return total

    return fold


def body(positions, normals, area, albedo, conductivity, soil, sun_tan, samples, occupancy):
    width = positions.shape[1]
    n_recv = lax.axis_size("recv")
    n_src = lax.axis_size("src")
    recv_index = lax.axis_index("recv")
    src_index = lax.axis_index("src")
    all_pos, all_nrm, all_area = (
        lax.all_gather(positions, ("recv", "src"), axis=1, tiled=True),
        lax.all_gather(normals, ("recv", "src"), axis=1, tiled=True),
        lax.all_gather(area, ("recv", "src"), axis=0, tiled=True),
    )
    horizon = horizons(all_pos, samples)
    facet_horizon = lax.all_to_all(
        horizon.astype(jnp.bfloat16), ("recv", "src"), split_axis=1, concat_axis=0, tiled=True
    ).astype(horizon.dtype)
    direct = sunlight(normals, sun_tan, facet_horizon)
    radiance = (albedo[None, :] * direct + emissivity * fourth(soil[0])[None, :]).astype(
        jnp.bfloat16
    )
    epochs = radiance.shape[0]
    table = occupancy.astype(jnp.float32)
    low_bits = recv_index % 4
    high_bits = recv_index // 4
    share = 4 * n_src
    rec_pos = lax.dynamic_slice_in_dim(all_pos, high_bits * share * width, share * width, 1)
    rec_nrm = lax.dynamic_slice_in_dim(all_nrm, high_bits * share * width, share * width, 1)
    mask_rows = lax.dynamic_slice_in_dim(table, high_bits * share, share, 0)
    column = low_bits * n_src + src_index

    def pick_class(values):
        lead = values.shape[:-1]
        arranged = values.reshape(lead + (n_recv // 4, share * width))
        chosen = lax.dynamic_slice_in_dim(arranged, column * width, width, len(lead) + 1)
        return chosen.reshape(lead + (n_recv // 4 * width,))

    def block_class(index):
        return index // width * share + column

    fold = make_fold(
        pick_class(all_pos),
        pick_class(all_nrm),
        pick_class(all_area),
        block_class,
        rec_pos,
        rec_nrm,
        mask_rows,
        width,
    )
    gathered = radiance
    for bit in range(2, n_recv.bit_length() - 1):
        other = partner(gathered, "recv", bit)
        upper = recv_index // (1 << bit) % 2 == 1
        gathered = jnp.where(
            upper, jnp.concatenate([other, gathered], 1), jnp.concatenate([gathered, other], 1)
        )
    start_sum = jnp.zeros((epochs, share * width), jnp.float32)
    partial_flux = fold(start_sum, gathered, jnp.int32(0))
    paired = lax.psum_scatter(
        partial_flux.reshape(epochs, 4, n_src, width), "src", scatter_dimension=2, tiled=True
    )
    paired = paired.reshape(epochs, 4, width)
    for bit in (1, 0):
        half = paired.shape[1] // 2
        lower = paired[:, :half]
        higher = paired[:, half:]
        upper = recv_index // (1 << bit) % 2 == 1
        keep = jnp.where(upper, higher, lower)
        outgoing = jnp.where(upper, lower, higher)
        paired = keep + partner(outgoing, "recv", bit)
    bounce = paired.reshape(epochs, width)
    final = conduct(soil, direct, bounce, albedo, conductivity)
    return (final, bounce)


def solution(mesh):
    in_specs = (
        P(None, ("basin", "recv", "src")),
        P(None, ("basin", "recv", "src")),
        P(("basin", "recv", "src")),
        P(("basin", "recv", "src")),
        P(("basin", "recv", "src")),
        P(None, ("basin", "recv", "src")),
        P(),
        P(("basin", "recv", "src"), None),
        P("basin", None),
    )
    out_specs = (P(None, ("basin", "recv", "src")), P(None, ("basin", "recv", "src")))
    return jax.shard_map(body, mesh=mesh, in_specs=in_specs, out_specs=out_specs, check_vma=False)
```

profile of v0, /device:TPU:0, one launch (start us, length us, event | category | flops | bytes accessed | tf_op | source)
XLA Modules:
  0.0 205.7 jit_solution(17961653555139462512)
XLA Ops:
  7.2 0.7 copy.50
  7.9 0.7 copy-done.6
  8.6 23.2 %all_gather.9 = f32[3,2048]{1,0:T(4,128)S(1)} all-gather(f32[3,128]{1,0:T(4,128)S(1)} %copy-done.6), channel_id=1, replica_groups=mesh['basin'=2,'recv'=8,'src'=2] {'recv','src'}, dimensions={1}, use_global_device_ids=true | all-gather | bytes 26112 | tf_op jit(solution)/shard_map/all_gather | solution.py:146
  32.5 91.5 %while.43 = (s32[]{:T(128)}, bf16[2048]{0:T(1024)(128)(2,1)S(1)}, s32[32]{0:T(128)S(1)}, f32[4096]{0:T(1024)S(1)}, f32[2048]{0:T(1024)S(1)}, /*index=5*/f32[4096...) while((s32[]{:T(128)}, bf16[2048]{0:T(1024)(128)(2,1)S(1)}, ...), condition=%wide.region_1.2_spmd.clone, body=%wide.region_0.1_spmd.clone.sunk | while | flops 24582 | bytes 57529 | solution.py:44
  35.3 0.7 dynamic_slice.136
  38.2 0.7 dynamic_slice.136
  41.0 0.7 dynamic_slice.136
  43.9 0.7 dynamic_slice.136
  46.7 0.7 dynamic_slice.136
  49.6 0.7 dynamic_slice.136
  124.5 3.5 %all-to-all-start = ((bf16[1,16,128]{2,0,1:T(2,128)(2,1)}), bf16[1,16,128]{2,0,1:T(2,128)(2,1)S(1)}, u32[]{:S(2)}, u32[]{:S(2)}) async-start(bf16[1,16,128]{2,0,1:T(2,128)(2,1)} %copy.16), calls=%async_computation | async-start | bytes 16384 | tf_op jit(solution)/shard_map/all_to_all | solution.py:151
  128.7 21.7 %all_gather.10 = f32[3,2048]{1,0:T(4,128)S(1)} all-gather(f32[3,128]{1,0:T(4,128)S(1)} %copy-done.5), channel_id=1, replica_groups=mesh['basin'=2,'recv'=8,'src'=2] {'recv','src'}, dimensions={1}, use_global_device_ids=true | all-gather | bytes 26112 | tf_op jit(solution)/shard_map/all_gather | solution.py:147
  152.0 17.4 %all-gather = f32[16,1,128]{2,1,0:T(1,128)S(1)} all-gather(f32[1,1,128]{2,1,0:T(1,128)S(1)} %bitcast.108), channel_id=1, replica_groups=mesh['basin'=2,'recv'=8,'src'=2] {'recv','src'}, dimensions={0}, use_global_device_ids=true | all-gather | bytes 8704 | tf_op jit(solution)/shard_map/all_gather | solution.py:148
  171.5 4.4 %collective-permute-done = bf16[16,128]{1,0:T(8,128)(2,1)S(1)} collective-permute-done((bf16[16,128]{1,0:T(8,128)(2,1)S(1)}, bf16[16,128]{1,0:T(8,128)(2,1)S(1)}, u32[]{:S(2)}, u32[]{:S(2)}) %collective-permute-start) | collective-permute-done | bytes 4128 | tf_op jit(solution)/shard_map/ppermute | solution.py:18
  175.9 5.1 %while.44 = (s32[]{:T(128)}, f32[16,1024]{1,0:T(8,128)S(1)}, s32[2]{0:T(128)S(1)}, bf16[16,256]{1,0:T(8,128)(2,1)S(1)}, f32[3,1024]{1,0:T(4,128)S(1)}, /*index=5...) while((s32[]{:T(128)}, f32[16,1024]{1,0:T(8,128)S(1)}, ...), condition=%wide.region_3.4_spmd.clone, body=%wide.region_2.3_spmd.clone.sunk | while | flops 8229127 | bytes 1284333 | solution.py:133
  177.6 0.8 convolution_add_fusion.2
  180.2 0.8 convolution_add_fusion.2
  181.7 6.1 %reduce-scatter.2.cloned.1.call-done = f32[16,4,1,128]{3,0,1,2:T(8,128)} async-done(((f32[16,4,2,128]{3,0,1,2:T(8,128)}), f32[16,4,1,128]{3,0,1,2:T(8,128)}) %reduce-scatter.2.cloned.1.call-update) | async-done | bytes 32784 | tf_op jit(solution)/shard_map/reduce_scatter | solution.py:196
  187.8 0.8 slice_select_fusion
  188.6 1.7 collective-permute-start.1
  190.3 2.1 %collective-permute-done.1 = f32[16,2,128]{2,0,1:T(8,128)S(1)} collective-permute-done((f32[16,2,128]{2,0,1:T(8,128)S(1)}, f32[16,2,128]{2,0,1:T(8,128)S(1)}, u32[]{:S(2)}, u32[]{:S(2)}) %collective-permute-start.1) | collective-permute-done | bytes 16416 | tf_op jit(solution)/shard_map/ppermute | solution.py:18
  192.4 1.7 collective-permute-start.2
  194.1 2.0 collective-permute-done.2
  196.7 1.5 while.42
  (212 shorter events, 30.9 us)
Async XLA Ops:
  7.9 0.7 copy-start.6
  31.8 0.7 copy-start.10
  124.5 46.0 %all-to-all-start = ((bf16[1,16,128]{2,0,1:T(2,128)(2,1)}), bf16[1,16,128]{2,0,1:T(2,128)(2,1)S(1)}, u32[]{:S(2)}, u32[]{:S(2)}) async-start(bf16[1,16,128]{2,0,1:T(2,128)(2,1)} %copy.16), calls=%async_computation | async-start | bytes 16384 | tf_op jit(solution)/shard_map/all_to_all | solution.py:151
  128.0 59.8 %reduce-scatter.2.cloned.1.call-start = ((), (), s32[]{:S(2)}) async-start(), calls=%async_computation.2 | async-start | bytes 98304 | tf_op jit(solution)/shard_map/reduce_scatter | solution.py:196
  128.1 0.7 copy-start.5
  150.5 0.7 copy-start.8
  150.5 0.7 copy-start.7
  151.3 0.7 copy-start.9
  170.6 0.7 copy-start.2
  171.3 4.6 %collective-permute-start = (bf16[16,128]{1,0:T(8,128)(2,1)S(1)}, bf16[16,128]{1,0:T(8,128)(2,1)S(1)}, u32[]{:S(2)}, u32[]{:S(2)}) collective-permute-start(bf16[16,128]{1,0:T(8,128)(2,1)S(1)} %get-tuple-element.374), channel_id=1, source_target_pairs={{0,8},{2,10},{4,12},{6,14},{8,0},{10,2},{12,4},{14,6},{1,9},{3,11}... | collective-permute-start | bytes 12296 | tf_op jit(solution)/shard_map/ppermute | solution.py:18
  187.8 4.5 %copy-start.1 = (f32[16,4,1,128]{3,0,1,2:T(8,128)S(1)}, f32[16,4,1,128]{3,0,1,2:T(8,128)}, u32[]{:S(2)}) copy-start(f32[16,4,1,128]{3,0,1,2:T(8,128)} %reduce-scatter.2.cloned.1.call-done) | copy-start | bytes 98308
  188.6 3.7 %collective-permute-start.1 = (f32[16,2,128]{2,0,1:T(8,128)S(1)}, f32[16,2,128]{2,0,1:T(8,128)S(1)}, u32[]{:S(2)}, u32[]{:S(2)}) collective-permute-start(f32[16,2,128]{2,0,1:T(8,128)S(1)} %slice_select_fusion), channel_id=1, source_target_pairs={{0,4},{2,6},{4,0},{6,2},{8,12},{10,14},{12,8},{14,10},{1,5},{3,7},... | collective-permute-start | bytes 49160 | tf_op jit(solution)/shard_map/ppermute | solution.py:18
  192.4 3.7 %collective-permute-start.2 = (f32[16,1,128]{2,0,1:T(8,128)S(1)}, f32[16,1,128]{2,0,1:T(8,128)S(1)}, u32[]{:S(2)}, u32[]{:S(2)}) collective-permute-start(f32[16,1,128]{2,0,1:T(8,128)S(1)} %slice_select_fusion.1), channel_id=1, source_target_pairs={{0,2},{2,0},{4,6},{6,4},{8,10},{10,8},{12,14},{14,12},{1,3},{3,1},... | collective-permute-start | bytes 24584 | tf_op jit(solution)/shard_map/ppermute | solution.py:18
  196.1 0.7 copy-start.4
  198.3 0.6 copy-start
  198.3 0.6 copy-start.3
Sparse Core Ops, SparseCore 0:
  181.8 5.9 reduce-scatter.1
where the time goes:
time: 207 us; the launch traced here: 206 us
  loops' own time  68.9 us (33%)
  blocking collectives  62.3 us (30%)
  local copies, waits for them, and re-layouts  31 us (15%)
  waiting for transfers between devices  14.5 us (7%)
  between operations  14.4 us (7%)
  starting transfers between devices  7 us (3%)
  other arithmetic  5.43 us (3%)
    another operation x1, loops' own time, profile_max(): best, unused = lax.scan(sweep, start, offsets)  67 us
    all_gather x1, blocking collectives, body(): lax.all_gather(positions, ('recv', 'src'), axis=1, tiled=True)  23.2 us
    all_gather x1, blocking collectives, body(): lax.all_gather(normals, ('recv', 'src'), axis=1, tiled=True)  21.7 us
    dynamic_slice x32, local copies, waits for them, and re-layouts, profile_max(): best, unused = lax.scan(sweep, start, offsets)  21.4 us
    all_gather x1, blocking collectives, body(): lax.all_gather(area, ('recv', 'src'), axis=0, tiled=True)  17.4 us
    ppermute x3, waiting for transfers between devices, partner(): return lax.ppermute(value, axis, pairs)  8.45 us
    reduce_scatter x1, waiting for transfers between devices, body(): lax.psum_scatter(partial_flux.reshape(epochs, 4, n_src, width), 'src', sc...  6.07 us
    unnamed x27, local copies, waits for them, and re-layouts  5.88 us
  transfers between devices with their start and end apart: 5, of which 4 were waited for; matrix products, arithmetic and copies ran while one was open for 1% of the time, Pallas kernels for 0%

commit v1 on v0

v1 whole, which is shorter than its diff:
```python
import functools
import math

import jax
import jax.numpy as jnp
from jax import lax
from jax.experimental import pallas as pl
from jax.experimental.pallas import tpu as pltpu
from jax.sharding import PartitionSpec as P

solar_flux = 2.0
emissivity = 0.9
surface_gain = 0.1
shade_width = 0.1
reach_offset = 0.05
GROUP = 8
CHUNK = 16


def fourth(value):
    square = value * value
    return square * square


def column(row, count):
    wide = jnp.broadcast_to(row[:, :count], (count, count))
    here = lax.broadcasted_iota(jnp.int32, (count, count), 0) == lax.broadcasted_iota(
        jnp.int32, (count, count), 1
    )
    return jnp.sum(jnp.where(here, wide, 0.0), axis=1, keepdims=True)


def kernel(
    n_recv,
    n_src,
    pos_ref,
    nrm_ref,
    area_ref,
    alb_ref,
    cond_ref,
    soil_ref,
    tan_ref,
    smp_ref,
    occ_ref,
    final_ref,
    bounce_ref,
    gath,
    planes,
    shifts,
    cols,
    view,
    direct_ref,
    radg,
    sems,
):
    n = n_recv * n_src
    width = pos_ref.shape[1]
    n_samples = smp_ref.shape[1]
    epochs = tan_ref.shape[1]
    layers = soil_ref.shape[0]
    bits = width.bit_length() - 1
    few = n <= 16
    me = lax.axis_index("recv") * n_src + lax.axis_index("src")

    def peer(k):
        p = lax.rem(me - k + n, n)
        return {"recv": p // n_src, "src": lax.rem(p, n_src)}

    def over(first, last, step):
        if few:
            for k in range(first, last):
                step(k)
        else:
            lax.fori_loop(first, last, lambda k, c: (step(k), c)[1], 0)

    barrier = pltpu.get_barrier_semaphore()
    over(
        1,
        n,
        lambda k: pl.semaphore_signal(
            barrier, inc=1, device_id=peer(k), device_id_type=pl.DeviceIdType.MESH
        ),
    )
    gath[0, 0:3, :] = pos_ref[...]
    gath[0, 3:6, :] = nrm_ref[...]
    gath[0, 6:7, :] = area_ref[...]
    gath[0, 7:8, 0:n_samples] = smp_ref[...].astype(jnp.float32)
    pl.semaphore_wait(barrier, n - 1)

    def send(ref, k, which):
        pltpu.make_async_remote_copy(
            src_ref=ref.at[0],
            dst_ref=ref.at[k],
            send_sem=sems.at[which],
            recv_sem=sems.at[which + 1],
            device_id=peer(k),
            device_id_type=pl.DeviceIdType.MESH,
        ).start()

    def everyone(ref, which):
        return pltpu.make_async_remote_copy(
            src_ref=ref.at[pl.ds(1, n - 1)],
            dst_ref=ref.at[pl.ds(1, n - 1)],
            send_sem=sems.at[which],
            recv_sem=sems.at[which + 1],
            device_id=peer(1),
            device_id_type=pl.DeviceIdType.MESH,
        )

    over(1, n, lambda k: send(gath, k, 0))

    mine = gath[0]
    tall = jnp.transpose(mine)
    for c in range(6):
        cols[c] = jnp.broadcast_to(tall[:, c : c + 1], (width, width))
    tan = column(tan_ref[...], epochs)
    angle = (
        2.0
        * math.pi
        * lax.broadcasted_iota(jnp.int32, (epochs, width), 0).astype(jnp.float32)
        / epochs
    )
    cos_e = 1.0 / jnp.sqrt(1.0 + tan * tan)
    incidence = (
        cos_e * jnp.cos(angle) * nrm_ref[0:1, :]
        + cos_e * jnp.sin(angle) * nrm_ref[1:2, :]
        + tan * cos_e * nrm_ref[2:3, :]
    )
    lit = solar_flux * jnp.maximum(incidence, 0.0)
    infrared = emissivity * fourth(soil_ref[0:1, :])

    everyone(gath, 0).wait_recv()
    for c in range(3):
        planes[c] = gath[:, c, :]
    rows = gath[:, 7, :]
    shifts[0:n, :] = rows
    shifts[n : 2 * n, :] = rows

    lane = lax.broadcasted_iota(jnp.int32, (GROUP, width), 1)
    px, py, pz = (jnp.broadcast_to(mine[c : c + 1, :], (GROUP, width)) for c in range(3))

    def azimuths(group):
        offset = n - me + group * GROUP
        steps = shifts[pl.ds(offset, GROUP), :].astype(jnp.int32)
        best = jnp.full((GROUP, width), -1e30, jnp.float32)
        for s in range(n_samples):
            shift = jnp.broadcast_to(steps[:, s : s + 1], (GROUP, width))
            row = ((shift + (width - 1) - lane) >> bits) & (n - 1)
            within = row & (GROUP - 1)
            part = row >> (GROUP.bit_length() - 1)
            turn = (lane + shift) & (width - 1)
            found = []
            for c in range(3):
                picked = None
                for g in range(n // GROUP):
                    block = planes[c, g * GROUP : (g + 1) * GROUP, :]
                    got = jnp.take_along_axis(block, within, axis=0)
                    picked = got if picked is None else jnp.where(part == g, got, picked)
                found.append(jnp.take_along_axis(picked, turn, axis=1))
            dx = found[0] - px
            dy = found[1] - py
            reach = jnp.sqrt(dx * dx + dy * dy) + reach_offset
            best = jnp.maximum(best, (found[2] - pz) / reach)
        start = group * GROUP
        direct_ref[pl.ds(start if few else pl.multiple_of(start, GROUP), GROUP), :] = best

    over(0, n // GROUP, azimuths)
    horizon = direct_ref[...]
    direct = lit * jax.nn.sigmoid((tan - horizon) / shade_width)
    direct_ref[...] = direct
    radg[0] = (alb_ref[...] * direct + infrared).astype(jnp.bfloat16)
    over(1, n, lambda k: send(radg, k, 2))

    def see(k, carry):
        block = gath[k]
        other = lax.rem(me + k, n)
        weight = occ_ref[me, other].astype(jnp.float32)
        sx, sy, sz, ox, oy, oz, size = (block[c : c + 1, :] for c in range(7))
        scale = size * weight / math.pi
        for i in range(width // CHUNK):
            at = slice(i * CHUNK, (i + 1) * CHUNK)
            dx = sx - cols[0, at, :]
            dy = sy - cols[1, at, :]
            dz = sz - cols[2, at, :]
            facing = cols[3, at, :] * dx + cols[4, at, :] * dy + cols[5, at, :] * dz
            toward = -(ox * dx + oy * dy + oz * dz)
            spread = dx * dx + dy * dy + dz * dz + size
            seen = jnp.maximum(facing, 0.0) * jnp.maximum(toward, 0.0) * scale
            view[k, at, :] = (seen / (spread * spread)).astype(jnp.bfloat16)
        return carry

    lax.fori_loop(0, n, see, 0)
    everyone(radg, 2).wait_recv()

    def fold(k, total):
        return total + lax.dot_general(
            radg[k], view[k], (((1,), (1,)), ((), ())), preferred_element_type=jnp.float32
        )

    total = jnp.zeros((epochs, width), jnp.float32)
    if few:
        for k in range(n):
            total = fold(k, total)
    else:
        total = lax.fori_loop(0, n, fold, total)
    bounce_ref[...] = total
    keep = surface_gain * (1.0 - alb_ref[...])
    direct_ref[...] = keep * (direct_ref[...] + total)
    cond = cond_ref[...]
    first = lax.broadcasted_iota(jnp.int32, (layers, width), 0) == 0
    last = lax.broadcasted_iota(jnp.int32, (layers, width), 0) == layers - 1

    def advance(t, temps):
        below = jnp.where(last, temps, pltpu.roll(temps, layers - 1, 0))
        above = jnp.where(first, temps, pltpu.roll(temps, 1, 0))
        temps = temps + cond * ((below - temps) - (temps - above))
        gain = direct_ref[pl.ds(t, 1), :] - (surface_gain * emissivity) * fourth(temps)
        return jnp.where(first, temps + gain, temps)

    temps = soil_ref[...]
    if few:
        for t in range(epochs):
            temps = advance(t, temps)
    else:
        temps = lax.fori_loop(0, epochs, advance, temps)
    final_ref[...] = temps
    everyone(gath, 0).wait_send()
    everyone(radg, 2).wait_send()


def body(positions, normals, area, albedo, conductivity, soil, sun_tan, samples, occupancy):
    n_recv = lax.axis_size("recv")
    n_src = lax.axis_size("src")
    n = n_recv * n_src
    width = positions.shape[1]
    epochs = sun_tan.shape[0]
    vmem = pl.BlockSpec(memory_space=pltpu.VMEM)
    return pl.pallas_call(
        functools.partial(kernel, n_recv, n_src),
        out_shape=(
            jax.ShapeDtypeStruct(soil.shape, jnp.float32),
            jax.ShapeDtypeStruct((epochs, width), jnp.float32),
        ),
        in_specs=[vmem] * 8 + [pl.BlockSpec(memory_space=pltpu.SMEM)],
        out_specs=(vmem, vmem),
        scratch_shapes=[
            pltpu.VMEM((n, 8, width), jnp.float32),
            pltpu.VMEM((3, n, width), jnp.float32),
            pltpu.VMEM((2 * n, width), jnp.float32),
            pltpu.VMEM((6, width, width), jnp.float32),
            pltpu.VMEM((n, width, width), jnp.bfloat16),
            pltpu.VMEM((epochs, width), jnp.float32),
            pltpu.VMEM((n, epochs, width), jnp.bfloat16),
            pltpu.SemaphoreType.DMA((4,)),
        ],
        compiler_params=pltpu.CompilerParams(collective_id=0, has_side_effects=True),
    )(
        positions,
        normals,
        area.reshape(1, width),
        albedo.reshape(1, width),
        conductivity.reshape(1, width),
        soil,
        sun_tan.reshape(1, epochs),
        samples,
        occupancy,
    )


def solution(mesh):
    in_specs = (
        P(None, ("basin", "recv", "src")),
        P(None, ("basin", "recv", "src")),
        P(("basin", "recv", "src")),
        P(("basin", "recv", "src")),
        P(("basin", "recv", "src")),
        P(None, ("basin", "recv", "src")),
        P(),
        P(("basin", "recv", "src"), None),
        P("basin", None),
    )
    out_specs = (P(None, ("basin", "recv", "src")), P(None, ("basin", "recv", "src")))
    return jax.shard_map(body, mesh=mesh, in_specs=in_specs, out_specs=out_specs, check_vma=False)
```

time: 207 us -> 21.8 us (0.11)
  loops' own time: 68.9 us -> 0 us
  blocking collectives: 62.3 us -> 0 us
  local copies, waits for them, and re-layouts: 31 us -> 1.93 us
  Pallas kernels: 0 us -> 19 us
  waiting for transfers between devices: 14.5 us -> 0 us
  between operations: 14.4 us -> 0.65 us
  starting transfers between devices: 7 us -> 0 us
  other arithmetic: 5.43 us -> 0 us
    another operation x3 -> x0, loops' own time: 68.9 us -> none  [the longest x1 67 us: profile_max(): best, unused = lax.scan(sweep, start, offsets)]
    all_gather x3 -> x0, blocking collectives: 62.3 us -> none  [the longest x1 23.2 us: body(): lax.all_gather(positions, ('recv', 'src'), axis=1, tiled=True)]
    dynamic_slice x40 -> x0, local copies, waits for them, and re-layouts: 22.7 us -> none  [the longest x32 21.4 us: profile_max(): best, unused = lax.scan(sweep, start, offsets)]
    pallas_call x0 -> x1, Pallas kernels: none -> 19 us  [body(): pl.pallas_call(functools.partial(kernel, n_recv, n_src), out_shape=(jax.S...]
    ppermute x3 -> x0, waiting for transfers between devices: 8.45 us -> none  [partner(): return lax.ppermute(value, axis, pairs)]
    reduce_scatter x1 -> x0, waiting for transfers between devices: 6.07 us -> none  [body(): lax.psum_scatter(partial_flux.reshape(epochs, 4, n_src, width), 'src', sc...]
    unnamed x27 -> x4, local copies, waits for them, and re-layouts: 5.88 us -> 1.93 us
    ppermute x3 -> x0, starting transfers between devices: 3.49 us -> none  [partner(): return lax.ppermute(value, axis, pairs)]
  transfers between devices with their start and end apart: 5 -> 0, of which waited for: 4 -> 0; matrix products, arithmetic and copies ran while one was open for 1% -> 0% of each run, Pallas kernels for 0% -> 0%
where the time goes in v1:
time: 21.8 us; the launch traced here: 21.5 us
  Pallas kernels  19 us (87%)
  local copies, waits for them, and re-layouts  1.93 us (9%)
  between operations  0.65 us (3%)
    pallas_call x1, Pallas kernels, body(): pl.pallas_call(functools.partial(kernel, n_recv, n_src), out_shape=(jax.S...  19 us
    unnamed x4, local copies, waits for them, and re-layouts  1.93 us

profile of v1, /device:TPU:0, one launch (start us, length us, event | category | flops | bytes accessed | tf_op | source)
XLA Modules:
  0.0 21.5 jit_solution(17473640584203456541)
XLA Ops:
  0.6 19.0 %shard_map.104 = (f32[32,128]{1,0:T(8,128)}, f32[16,128]{1,0:T(8,128)}) custom-call(f32[3,128]{1,0:T(4,128)} %pos_ref.1, f32[3,128]{1,0:T(4,128)} %nrm_ref.1, f32[1,128]{1,0:T(1,128)} %bitcast.4, f32[1,128]{1,0:T(1,128)} %bitcast.5, f32[1,128]{1,0:T(1,128)} %bitcast.6, f32[32,128]{1,0:T(8,128)} %soil_ref.1, f32[1,16]{1,0:T(1,128)} %bitcast.7, ...), custom_call_target="tpu_custom_call" | custom-call | tf_op jit(solution)/shard_map/pallas_call | solution.py:238
  19.6 0.0 copy-start
  19.6 1.3 %copy.13 = f32[32,128]{1,0:T(8,128)} copy(f32[32,128]{1,0:T(8,128)} %get-tuple-element.4) | data formatting | bytes 32768
  20.9 0.0 copy-done
  20.9 0.6 %copy.14 = f32[16,128]{1,0:T(8,128)} copy(f32[16,128]{1,0:T(8,128)S(1)} %copy-done) | data formatting | bytes 16384
Async XLA Ops:
  19.6 1.3 %copy-start = (f32[16,128]{1,0:T(8,128)S(1)}, f32[16,128]{1,0:T(8,128)}, u32[]{:S(2)}) copy-start(f32[16,128]{1,0:T(8,128)} %get-tuple-element.5) | copy-start | bytes 24580

commit v2 on v1

--- a/solution.py
+++ b/solution.py
@@ -33,18 +33,28 @@
 def kernel(
     n_recv,
     n_src,
+    pos_in,
+    nrm_in,
+    area_in,
+    alb_in,
+    cond_in,
+    soil_in,
+    tan_in,
+    smp_in,
+    occ_in,
+    bounce_ref,
+    heat_ref,
+    cond_ref,
+    soil_ref,
     pos_ref,
     nrm_ref,
     area_ref,
     alb_ref,
-    cond_ref,
-    soil_ref,
     tan_ref,
     smp_ref,
     occ_ref,
-    final_ref,
-    bounce_ref,
-    gath,
+    near,
+    far,
     planes,
     shifts,
     cols,
@@ -52,12 +62,12 @@
     direct_ref,
     radg,
     sems,
+    loads,
 ):
     n = n_recv * n_src
     width = pos_ref.shape[1]
     n_samples = smp_ref.shape[1]
     epochs = tan_ref.shape[1]
-    layers = soil_ref.shape[0]
     bits = width.bit_length() - 1
     few = n <= 16
     me = lax.axis_index("recv") * n_src + lax.axis_index("src")
@@ -68,7 +78,7 @@
 
     def over(first, last, step):
         if few:
-            for k in range(first, last):
+            for k in sorted(range(first, last), key=lambda k: abs(2 * k - n)):
                 step(k)
         else:
             lax.fori_loop(first, last, lambda k, c: (step(k), c)[1], 0)
@@ -81,10 +91,30 @@
             barrier, inc=1, device_id=peer(k), device_id_type=pl.DeviceIdType.MESH
         ),
     )
-    gath[0, 0:3, :] = pos_ref[...]
-    gath[0, 3:6, :] = nrm_ref[...]
-    gath[0, 6:7, :] = area_ref[...]
-    gath[0, 7:8, 0:n_samples] = smp_ref[...].astype(jnp.float32)
+    pairs = (
+        (pos_in, pos_ref),
+        (smp_in, smp_ref),
+        (nrm_in, nrm_ref),
+        (area_in, area_ref),
+        (tan_in, tan_ref),
+        (soil_in, soil_ref),
+        (alb_in, alb_ref),
+        (cond_in, cond_ref),
+        (occ_in.at[pl.ds(me, 1)], occ_ref),
+    )
+    fetched = [
+        pltpu.make_async_copy(there, here, loads.at[i]) for i, (there, here) in enumerate(pairs)
+    ]
+    for copy in fetched:
+        copy.start()
+    for copy in fetched[:4]:
+        copy.wait()
+    near[0, 0:3, :] = pos_ref[...]
+    near[0, 3:4, 0:n_samples] = smp_ref[...].astype(jnp.float32)
+    far[0, 0:3, :] = nrm_ref[...]
+    far[0, 3:4, :] = area_ref[...]
+    for copy in fetched[4:]:
+        copy.wait()
     pl.semaphore_wait(barrier, n - 1)
 
     def send(ref, k, which):
@@ -107,12 +137,13 @@
             device_id_type=pl.DeviceIdType.MESH,
         )
 
-    over(1, n, lambda k: send(gath, k, 0))
-
-    mine = gath[0]
-    tall = jnp.transpose(mine)
-    for c in range(6):
-        cols[c] = jnp.broadcast_to(tall[:, c : c + 1], (width, width))
+    over(1, n, lambda k: send(near, k, 0))
+    over(1, n, lambda k: send(far, k, 4))
+
+    mine = near[0]
+    tall = jnp.transpose(jnp.concatenate([mine, far[0]], axis=0))
+    for c, at in enumerate((0, 1, 2, 4, 5, 6)):
+        cols[c] = jnp.broadcast_to(tall[:, at : at + 1], (width, width))
     tan = column(tan_ref[...], epochs)
     angle = (
         2.0
@@ -129,10 +160,10 @@
     lit = solar_flux * jnp.maximum(incidence, 0.0)
     infrared = emissivity * fourth(soil_ref[0:1, :])
 
-    everyone(gath, 0).wait_recv()
+    everyone(near, 0).wait_recv()
     for c in range(3):
-        planes[c] = gath[:, c, :]
-    rows = gath[:, 7, :]
+        planes[c] = near[:, c, :]
+    rows = near[:, 3, :]
     shifts[0:n, :] = rows
     shifts[n : 2 * n, :] = rows
 
@@ -172,10 +203,9 @@
     over(1, n, lambda k: send(radg, k, 2))
 
     def see(k, carry):
-        block = gath[k]
-        other = lax.rem(me + k, n)
-        weight = occ_ref[me, other].astype(jnp.float32)
-        sx, sy, sz, ox, oy, oz, size = (block[c : c + 1, :] for c in range(7))
+        weight = occ_ref[0, lax.rem(me + k, n)].astype(jnp.float32)
+        sx, sy, sz = (near[k, c : c + 1, :] for c in range(3))
+        ox, oy, oz, size = (far[k, c : c + 1, :] for c in range(4))
         scale = size * weight / math.pi
         for i in range(width // CHUNK):
             at = slice(i * CHUNK, (i + 1) * CHUNK)
@@ -189,6 +219,7 @@
             view[k, at, :] = (seen / (spread * spread)).astype(jnp.bfloat16)
         return carry
 
+    everyone(far, 4).wait_recv()
     lax.fori_loop(0, n, see, 0)
     everyone(radg, 2).wait_recv()
 
@@ -205,7 +236,16 @@
         total = lax.fori_loop(0, n, fold, total)
     bounce_ref[...] = total
     keep = surface_gain * (1.0 - alb_ref[...])
-    direct_ref[...] = keep * (direct_ref[...] + total)
+    heat_ref[...] = keep * (direct_ref[...] + total)
+    everyone(near, 0).wait_send()
+    everyone(far, 4).wait_send()
+    everyone(radg, 2).wait_send()
+
+
+def conduct(bounce_in, heat_ref, cond_ref, soil_ref, final_ref, bounce_ref):
+    layers, width = soil_ref.shape
+    epochs = heat_ref.shape[0]
+    bounce_ref[...] = bounce_in[...]
     cond = cond_ref[...]
     first = lax.broadcasted_iota(jnp.int32, (layers, width), 0) == 0
     last = lax.broadcasted_iota(jnp.int32, (layers, width), 0) == layers - 1
@@ -214,18 +254,16 @@
         below = jnp.where(last, temps, pltpu.roll(temps, layers - 1, 0))
         above = jnp.where(first, temps, pltpu.roll(temps, 1, 0))
         temps = temps + cond * ((below - temps) - (temps - above))
-        gain = direct_ref[pl.ds(t, 1), :] - (surface_gain * emissivity) * fourth(temps)
+        gain = heat_ref[pl.ds(t, 1), :] - (surface_gain * emissivity) * fourth(temps)
         return jnp.where(first, temps + gain, temps)
 
     temps = soil_ref[...]
-    if few:
+    if epochs <= 16:
         for t in range(epochs):
             temps = advance(t, temps)
     else:
         temps = lax.fori_loop(0, epochs, advance, temps)
     final_ref[...] = temps
-    everyone(gath, 0).wait_send()
-    everyone(radg, 2).wait_send()
 
 
 def body(positions, normals, area, albedo, conductivity, soil, sun_tan, samples, occupancy):
@@ -235,23 +273,36 @@
     width = positions.shape[1]
     epochs = sun_tan.shape[0]
     vmem = pl.BlockSpec(memory_space=pltpu.VMEM)
-    return pl.pallas_call(
+    f32 = jnp.float32
+    n_samples = samples.shape[1]
+    held = pl.pallas_call(
         functools.partial(kernel, n_recv, n_src),
         out_shape=(
-            jax.ShapeDtypeStruct(soil.shape, jnp.float32),
-            jax.ShapeDtypeStruct((epochs, width), jnp.float32),
+            pltpu.VMEM((epochs, width), f32),
+            pltpu.VMEM((epochs, width), f32),
+            pltpu.VMEM((1, width), f32),
+            pltpu.VMEM(soil.shape, f32),
         ),
-        in_specs=[vmem] * 8 + [pl.BlockSpec(memory_space=pltpu.SMEM)],
-        out_specs=(vmem, vmem),
+        in_specs=[pl.BlockSpec(memory_space=pl.ANY)] * 9,
+        out_specs=(vmem,) * 4,
         scratch_shapes=[
-            pltpu.VMEM((n, 8, width), jnp.float32),
-            pltpu.VMEM((3, n, width), jnp.float32),
-            pltpu.VMEM((2 * n, width), jnp.float32),
-            pltpu.VMEM((6, width, width), jnp.float32),
+            pltpu.VMEM((3, width), f32),
+            pltpu.VMEM((3, width), f32),
+            pltpu.VMEM((1, width), f32),
+            pltpu.VMEM((1, width), f32),
+            pltpu.VMEM((1, epochs), f32),
+            pltpu.VMEM((1, n_samples), jnp.int32),
+            pltpu.SMEM((1, occupancy.shape[1]), jnp.int32),
+            pltpu.VMEM((n, 4, width), f32),
+            pltpu.VMEM((n, 4, width), f32),
+            pltpu.VMEM((3, n, width), f32),
+            pltpu.VMEM((2 * n, width), f32),
+            pltpu.VMEM((6, width, width), f32),
             pltpu.VMEM((n, width, width), jnp.bfloat16),
-            pltpu.VMEM((epochs, width), jnp.float32),
+            pltpu.VMEM((epochs, width), f32),
             pltpu.VMEM((n, epochs, width), jnp.bfloat16),
-            pltpu.SemaphoreType.DMA((4,)),
+            pltpu.SemaphoreType.DMA((6,)),
+            pltpu.SemaphoreType.DMA((9,)),
         ],
         compiler_params=pltpu.CompilerParams(collective_id=0, has_side_effects=True),
     )(
@@ -265,6 +316,15 @@
         samples,
         occupancy,
     )
+    return pl.pallas_call(
+        conduct,
+        out_shape=(
+            jax.ShapeDtypeStruct(soil.shape, f32),
+            jax.ShapeDtypeStruct((epochs, width), f32),
+        ),
+        in_specs=[vmem] * 4,
+        out_specs=(vmem, vmem),
+    )(*(pltpu.with_memory_space_constraint(value, pltpu.VMEM) for value in held))
 
 
 def solution(mesh):

time: 21.8 us -> 19.1 us (0.88)
  local copies, waits for them, and re-layouts: 1.93 us -> 0 us
  Pallas kernels: 19 us -> 18.3 us
    unnamed x4 -> x0, local copies, waits for them, and re-layouts: 1.93 us -> none
    pallas_call x1 -> x2, Pallas kernels: 19 us -> 18.3 us  [the longest x1 17.5 us: body(): pl.pallas_call(functools.partial(kernel, n_recv, n_src), out_shape=(pltpu...]
where the time goes in v2:
time: 19.1 us; the launch traced here: 18.9 us
  Pallas kernels  18.3 us (96%)
  between operations  0.64 us (3%)
    pallas_call x1, Pallas kernels, body(): pl.pallas_call(functools.partial(kernel, n_recv, n_src), out_shape=(pltpu...  17.5 us
    pallas_call x1, Pallas kernels, body(): pl.pallas_call(conduct, out_shape=(jax.ShapeDtypeStruct(soil.shape, f32),...  0.81 us

profile of v2, /device:TPU:0, one launch (start us, length us, event | category | flops | bytes accessed | tf_op | source)
XLA Modules:
  0.0 18.9 jit_solution(4765497422317552961)
XLA Ops:
  0.6 17.5 %shard_map.104 = (f32[16,128]{1,0:T(8,128)S(1)}, f32[16,128]{1,0:T(8,128)S(1)}, f32[1,128]{1,0:T(1,128)S(1)}, f32[32,128]{1,0:T(8,128)S(1)}) custom-call(f32[3,128]{1,0:T(4,128)} %pos_in.1, f32[3,128]{1,0:T(4,128)} %nrm_in.1, f32[1,128]{1,0:T(1,128)} %bitcast.4, f32[1,128]{1,0:T(1,128)} %bitcast.5, f32[1,128]{1,0:T(1,128)} %bitcast.6, f32[32,128]{1,0:T(8,128)} %soil_in.1, ...), custom_call_target="tpu_custom_call" | custom-call | tf_op jit(solution)/shard_map/pallas_call | solution.py:278
  18.1 0.8 %shard_map.105 = (f32[32,128]{1,0:T(8,128)}, f32[16,128]{1,0:T(8,128)}) custom-call(f32[16,128]{1,0:T(8,128)S(1)} %get-tuple-element.6.bounce_in, f32[16,128]{1,0:T(8,128)S(1)} %get-tuple-element.7.heat_ref, f32[1,128]{1,0:T(1,128)S(1)} %get-tuple-element.8.cond_ref, f32[32,128]{1,0:T(8,128)S(1)} %get-tuple-element.9.soil_ref), custom_call_target="tpu_custom_call" | custom-call | tf_op jit(solution)/shard_map/pallas_call | solution.py:319

commit v3 on v2

--- a/solution.py
+++ b/solution.py
@@ -60,6 +60,8 @@
     cols,
     view,
     direct_ref,
+    lit_ref,
+    tall_tan,
     radg,
     sems,
     loads,
@@ -73,8 +75,8 @@
     me = lax.axis_index("recv") * n_src + lax.axis_index("src")
 
     def peer(k):
-        p = lax.rem(me - k + n, n)
-        return {"recv": p // n_src, "src": lax.rem(p, n_src)}
+        p = (me + (n - k)) & (n - 1)
+        return {"recv": p >> (n_src.bit_length() - 1), "src": p & (n_src - 1)}
 
     def over(first, last, step):
         if few:
@@ -157,7 +159,8 @@
         + cos_e * jnp.sin(angle) * nrm_ref[1:2, :]
         + tan * cos_e * nrm_ref[2:3, :]
     )
-    lit = solar_flux * jnp.maximum(incidence, 0.0)
+    lit_ref[...] = solar_flux * jnp.maximum(incidence, 0.0)
+    tall_tan[...] = jnp.broadcast_to(tan, (epochs, width))
     infrared = emissivity * fourth(soil_ref[0:1, :])
 
     everyone(near, 0).wait_recv()
@@ -193,14 +196,13 @@
             reach = jnp.sqrt(dx * dx + dy * dy) + reach_offset
             best = jnp.maximum(best, (found[2] - pz) / reach)
         start = group * GROUP
-        direct_ref[pl.ds(start if few else pl.multiple_of(start, GROUP), GROUP), :] = best
+        here = pl.ds(start if few else pl.multiple_of(start, GROUP), GROUP)
+        direct = lit_ref[here, :] * jax.nn.sigmoid((tall_tan[here, :] - best) / shade_width)
+        direct_ref[here, :] = direct
+        radg[0, group] = (alb_ref[...] * direct + infrared).astype(jnp.bfloat16)
+        over(1, n, lambda k: send(radg.at[:, group], k, 2))
 
     over(0, n // GROUP, azimuths)
-    horizon = direct_ref[...]
-    direct = lit * jax.nn.sigmoid((tan - horizon) / shade_width)
-    direct_ref[...] = direct
-    radg[0] = (alb_ref[...] * direct + infrared).astype(jnp.bfloat16)
-    over(1, n, lambda k: send(radg, k, 2))
 
     def see(k, carry):
         weight = occ_ref[0, lax.rem(me + k, n)].astype(jnp.float32)
@@ -224,8 +226,9 @@
     everyone(radg, 2).wait_recv()
 
     def fold(k, total):
+        sent = jnp.concatenate([radg[k, g] for g in range(epochs // GROUP)], axis=0)
         return total + lax.dot_general(
-            radg[k], view[k], (((1,), (1,)), ((), ())), preferred_element_type=jnp.float32
+            sent, view[k], (((1,), (1,)), ((), ())), preferred_element_type=jnp.float32
         )
 
     total = jnp.zeros((epochs, width), jnp.float32)
@@ -300,7 +303,9 @@
             pltpu.VMEM((6, width, width), f32),
             pltpu.VMEM((n, width, width), jnp.bfloat16),
             pltpu.VMEM((epochs, width), f32),
-            pltpu.VMEM((n, epochs, width), jnp.bfloat16),
+            pltpu.VMEM((epochs, width), f32),
+            pltpu.VMEM((epochs, width), f32),
+            pltpu.VMEM((n, epochs // GROUP, GROUP, width), jnp.bfloat16),
             pltpu.SemaphoreType.DMA((6,)),
             pltpu.SemaphoreType.DMA((9,)),
         ],

time: 19.1 us -> 17.6 us (0.921)
  Pallas kernels: 18.3 us -> 16.7 us
    pallas_call x1, Pallas kernels: 17.5 us -> 15.9 us  [body(): pl.pallas_call(functools.partial(kernel, n_recv, n_src), out_shape=(pltpu...]
where the time goes in v3:
time: 17.6 us; the launch traced here: 17.4 us
  Pallas kernels  16.7 us (95%)
  between operations  0.64 us (4%)
    pallas_call x1, Pallas kernels, body(): pl.pallas_call(functools.partial(kernel, n_recv, n_src), out_shape=(pltpu...  15.9 us
    pallas_call x1, Pallas kernels, body(): pl.pallas_call(conduct, out_shape=(jax.ShapeDtypeStruct(soil.shape, f32),...  0.81 us

profile of v3, /device:TPU:0, one launch (start us, length us, event | category | flops | bytes accessed | tf_op | source)
XLA Modules:
  0.0 17.4 jit_solution(3611295210618017264)
XLA Ops:
  0.6 15.9 %shard_map.104 = (f32[16,128]{1,0:T(8,128)S(1)}, f32[16,128]{1,0:T(8,128)S(1)}, f32[1,128]{1,0:T(1,128)S(1)}, f32[32,128]{1,0:T(8,128)S(1)}) custom-call(f32[3,128]{1,0:T(4,128)} %pos_in.1, f32[3,128]{1,0:T(4,128)} %nrm_in.1, f32[1,128]{1,0:T(1,128)} %bitcast.4, f32[1,128]{1,0:T(1,128)} %bitcast.5, f32[1,128]{1,0:T(1,128)} %bitcast.6, f32[32,128]{1,0:T(8,128)} %soil_in.1, ...), custom_call_target="tpu_custom_call" | custom-call | tf_op jit(solution)/shard_map/pallas_call | solution.py:281
  16.6 0.8 %shard_map.105 = (f32[32,128]{1,0:T(8,128)}, f32[16,128]{1,0:T(8,128)}) custom-call(f32[16,128]{1,0:T(8,128)S(1)} %get-tuple-element.6.bounce_in, f32[16,128]{1,0:T(8,128)S(1)} %get-tuple-element.7.heat_ref, f32[1,128]{1,0:T(1,128)S(1)} %get-tuple-element.8.cond_ref, f32[32,128]{1,0:T(8,128)S(1)} %get-tuple-element.9.soil_ref), custom_call_target="tpu_custom_call" | custom-call | tf_op jit(solution)/shard_map/pallas_call | solution.py:324
